TPU v7x, 32 devices: a whole 2x2x4 slice. The times are simulated.
32 devices in a mesh: row: 4 (over z), col: 8 (over y, x, core).
Axes of the slice: x: 2, y: 2, z: 4, core: 2. Of those that a mesh axis runs over, the one named last changes fastest.
Arguments:
- air_flux: bfloat16 [4, 4096, 16, 128], P(None, ('row', 'col')), may hold values from -1 to 3
- air_area: float32 [4096, 128], P(('row', 'col')), may hold values from 0.2 to 2
- sea_area: float32 [4096, 128], P(('row', 'col')), may hold values from 0.2 to 2
- wet_mask: int32 [4096], P(('row', 'col')), may hold values 0 or 1
- intersection_tiles: bfloat16 [32, 128, 128], replicated, may hold values from -0.125 to 0.125
- send_block: int32 [32, 256], P(('row', 'col')), may hold values from 0 to 127
- target_slot: int32 [4096, 16], P(('row', 'col')), may hold values from 0 to 255
- target_tile: int32 [4096, 16], P(('row', 'col')), may hold values from 0 to 31, as said below
Outputs:
- sea_flux: float32 [4096, 16, 128], P(('row', 'col'))
Inputs may be any that keep to these rules, and one draw needn't show every extreme that they name: `target_tile`: the 16 entries of a row are distinct.
All inputs are finite; a program needn't handle non-finite values. No bound on the sum of `wet_mask` on one device may be relied on, other than what follows from the above.
Results may differ from a plain program's by a relative error of at most 0.0003.
The roundings to bfloat16 on the way count: a program that leaves them out, or rounds other values in their place, can miss the bound.
Values may be sent and summed in bfloat16 or wider, within the bound.
No kernel may reach another device: no remote copies, remote signals or barrier semaphores. Data moves between devices by JAX's collectives and lax.ppermute only.
A program may use at most 128 MiB of HBM per device.

v0:
```python
import jax
import jax.numpy as jnp
from jax import lax
from jax.sharding import PartitionSpec as P

NSTEPS = 4


def regrid_fields(source_rows, row_index, tile_index, intersection_tiles):
    targets = tile_index.shape[0]
    intersections = tile_index.shape[1]
    fields = source_rows.shape[1]
    cell_count = source_rows.shape[2]
    picked = jnp.take(source_rows, row_index.reshape(-1), axis=0).reshape(
        targets, intersections, fields, cell_count
    )
    tile_ids = jnp.arange(intersection_tiles.shape[0], dtype=jnp.int32)
    onehot = (tile_index[:, :, None] == tile_ids[None, None, :]).astype(jnp.bfloat16)
    grouped = jnp.einsum(
        "tkw,tkfc->twfc", onehot, picked, preferred_element_type=jnp.float32
    ).astype(jnp.bfloat16)
    return jnp.einsum(
        "twfc,wcd->tfd", grouped, intersection_tiles, preferred_element_type=jnp.float32
    )


def body(
    air_flux, air_area, sea_area, wet_mask, intersection_tiles, send_block, target_slot, target_tile
):
    mean_flux = jnp.sum(air_flux, axis=0, dtype=jnp.float32) / NSTEPS
    sent_flux = mean_flux.astype(jnp.bfloat16)
    air_part = jnp.sum(mean_flux * air_area[:, None, :], axis=(0, 2))
    air_total = lax.psum(air_part, ("row", "col"))
    outbound = jnp.take(sent_flux, send_block[0], axis=0)
    raw_flux = regrid_fields(
        lax.all_to_all(outbound, "col", split_axis=0, concat_axis=0, tiled=True),
        target_slot,
        target_tile,
        intersection_tiles,
    )
    wet_float = wet_mask.astype(jnp.float32)
    wet_area = wet_float[:, None] * sea_area
    sea_part = jnp.sum(raw_flux * wet_area[:, None, :], axis=(0, 2))
    wet_part = jnp.sum(wet_area)
    sea_total, wet_sum = lax.psum((sea_part, wet_part), ("row", "col"))
    shift = (air_total - sea_total) / jnp.maximum(wet_sum, 1.0)
    return wet_float[:, None, None] * (raw_flux + shift[None, :, None])


def solution(mesh):
    placed = (
        P(None, ("row", "col"), None, None),
        P(("row", "col"), None),
        P(("row", "col"), None),
        P(("row", "col")),
        P(),
        P(("row", "col"), None),
        P(("row", "col"), None),
        P(("row", "col"), None),
    )
    return jax.shard_map(
        body, mesh=mesh, in_specs=placed, out_specs=P(("row", "col"), None, None), check_vma=False
    )
```

profile of v0, /device:TPU:0, one launch (start us, length us, event | category | flops | bytes accessed | tf_op | source)
XLA Modules:
  0.0 115.9 jit_solution(8608368607367261870)
XLA Ops:
  0.0 0.0 copy-start
  0.0 0.0 copy-start.2
  0.0 0.0 copy-start.4
  0.0 0.0 copy-start.3
  0.0 0.0 copy-start.1
  0.0 0.8 compare_select_fusion.2
  0.8 0.7 compare_and_fusion.1
  1.5 0.8 broadcast_multiply_fusion.1
  2.3 2.0 %convert_reduce_fusion = f32[128,16,128]{2,1,0:T(8,128)S(1)} fusion(bf16[4,128,16,128]{3,2,1,0:T(8,128)(2,1)} %param.8), kind=kLoop, calls=%fused_computation.8 | loop fusion | flops 1835008 | bytes 3145728 | tf_op jit(solution)/shard_map/reduce_sum | solution.py:30
  4.4 0.3 multiply_reduce_fusion.1
  4.7 0.9 gather_fusion
  5.5 1.7 %broadcast_select_fusion = bf16[256,16,128]{2,1,0:T(8,128)(2,1)} fusion(bf16[256,16,128]{2,1,0:T(8,128)(2,1)S(1)} %gather_fusion, pred[256]{0:T(512)(128)(4,1)S(1)} %compare_and_fusion.1), kind=kLoop, calls=%fused_computation.16 | loop fusion | flops 524288 | bytes 2097408 | tf_op jit(solution)/shard_map/jit(_take)/select_n | solution.py:34
  7.3 5.2 %all-to-all-start = ((bf16[256,16,128]{2,1,0:T(8,128)(2,1)}), bf16[256,16,128]{2,1,0:T(8,128)(2,1)S(1)}, u32[]{:S(2)}, u32[]{:S(2)}) async-start(bf16[256,16,128]{2,1,0:T(8,128)(2,1)} %broadcast_select_fusion), calls=%async_computation | async-start | bytes 2097152 | tf_op jit(solution)/shard_map/all_to_all | solution.py:36
  12.5 0.0 copy-done.2
  12.5 0.1 copy.18
  12.6 0.0 copy-done.4
  12.6 0.1 copy.17
  12.7 0.0 copy-done.3
  12.7 0.1 copy.16
  12.8 0.1 reshape.80
  13.0 0.0 copy-done.1
  13.0 0.7 fusion.12
  13.7 14.2 %all-to-all-done = bf16[256,16,128]{2,1,0:T(8,128)(2,1)S(1)} async-done(((bf16[256,16,128]{2,1,0:T(8,128)(2,1)}), bf16[256,16,128]{2,1,0:T(8,128)(2,1)S(1)}, u32[]{:S(2)}, u32[]{:S(2)}) %all-to-all-start) | async-done | bytes 1048608 | tf_op jit(solution)/shard_map/all_to_all | solution.py:36
  27.8 16.3 %gather_fusion.1 = bf16[2048,16,128]{2,1,0:T(8,128)(2,1)} fusion(bf16[256,16,128]{2,1,0:T(8,128)(2,1)S(1)} %all-to-all-done, s32[2048]{0:T(1024)S(1)} %broadcast_clamp_fusion), kind=kCustom, calls=%fused_computation.1 | custom fusion | bytes 16785408 | tf_op jit(solution)/shard_map/jit(_take)/gather | solution.py:14
  44.1 12.9 %convolution_convert_fusion = bf16[128,32,16,128]{3,1,2,0:T(8,128)(2,1)} fusion(bf16[128,16,16,128]{3,2,1,0:T(8,128)(2,1)} %bitcast.19, pred[128,16]{1,0:T(8,128)(4,1)S(1)} %copy.17, s32[128,16]{1,0:T(8,128)S(1)} %copy.16), kind=kOutput, calls=%fused_computation.4 | convolution fusion | flops 281083904 | bytes 25176064 | tf_op jit(solution)/shard_map/tkw,tkfc->twfc/dot_general | solution.py:19
  57.0 0.0 copy-done
  57.0 16.8 %multiply_reduce_fusion = (f32[16]{0:T(128)S(1)}, f32[128,16,128]{2,0,1:T(8,128)S(1)}) fusion(f32[128,128]{1,0:T(8,128)S(1)} %get-tuple-element.9, bf16[32,128,128]{2,1,0:T(8,128)(2,1)S(1)} %copy-done, bf16[128,32,16,128]{3,1,2,0:T(8,128)(2,1)} %convolution_convert_fusion), kind=kOutput, calls=%fused_computation.12 | convolution fusion | flops 2148007936 | bytes 18939968 | tf_op jit(solution)/shard_map/twfc,wcd->tfd/dot_general | solution.py:22
  73.8 39.6 %all-reduce = (f32[16]{0:T(128)S(1)}, f32[16]{0:T(128)S(1)}, f32[]{:T(128)}) all-reduce(f32[16]{0:T(128)S(1)} %get-tuple-element.10, f32[16]{0:T(128)S(1)} %get-tuple-element.12, f32[]{:T(128)} %get-tuple-element.8), channel_id=1, replica_groups=mesh['row'=4,'col'=8] {'row','col'}, use_global_device_ids=true, to_apply=%region_2.0 | all-reduce | flops 33 | bytes 264 | tf_op jit(solution)/shard_map/psum | solution.py:33
  114.1 0.2 add_multiply_fusion
  114.3 1.6 %copy.21 = f32[128,16,128]{2,1,0:T(8,128)} copy(f32[128,16,128]{2,0,1:T(8,128)S(1)} %add_multiply_fusion) | data formatting | bytes 2097152 | tf_op jit(solution)/shard_map/mul | solution.py:47
  (6 shorter events, 0.0 us)
Async XLA Ops:
  0.0 57.0 %copy-start = (bf16[32,128,128]{2,1,0:T(8,128)(2,1)S(1)}, bf16[32,128,128]{2,1,0:T(8,128)(2,1)}, u32[]{:S(2)}) copy-start(bf16[32,128,128]{2,1,0:T(8,128)(2,1)} %param.12) | copy-start | bytes 3145732
  0.0 12.5 %copy-start.2 = (s32[128,16]{0,1:T(8,128)S(1)}, s32[128,16]{0,1:T(8,128)}, u32[]{:S(2)}) copy-start(s32[128,16]{0,1:T(8,128)} %param.14) | copy-start | bytes 24580
  0.0 12.6 %copy-start.4 = (s32[128]{0:T(128)S(1)}, s32[128]{0:T(128)}, u32[]{:S(2)}) copy-start(s32[128]{0:T(128)} %param.11) | copy-start | bytes 1540
  0.0 12.7 %copy-start.3 = (s32[128,16]{0,1:T(8,128)S(1)}, s32[128,16]{0,1:T(8,128)}, u32[]{:S(2)}) copy-start(s32[128,16]{0,1:T(8,128)} %param.15) | copy-start | bytes 24580
  0.0 12.9 %copy-start.1 = (f32[128,128]{1,0:T(8,128)S(1)}, f32[128,128]{1,0:T(8,128)}, u32[]{:S(2)}) copy-start(f32[128,128]{1,0:T(8,128)} %param.10) | copy-start | bytes 196612
  7.3 20.6 %all-to-all-start = ((bf16[256,16,128]{2,1,0:T(8,128)(2,1)}), bf16[256,16,128]{2,1,0:T(8,128)(2,1)S(1)}, u32[]{:S(2)}, u32[]{:S(2)}) async-start(bf16[256,16,128]{2,1,0:T(8,128)(2,1)} %broadcast_select_fusion), calls=%async_computation | async-start | bytes 2097152 | tf_op jit(solution)/shard_map/all_to_all | solution.py:36
where the time goes:
time: 116 us
  blocking collectives  39.6 us (34%)
  matrix products  29.7 us (26%)
  local copies, waits for them, and re-layouts  19.1 us (16%)
  waiting for transfers between devices  14.2 us (12%)
  other arithmetic  7.32 us (6%)
  starting transfers between devices  5.2 us (4%)
    psum x1, blocking collectives, body(): air_total = lax.psum(air_part, ('row', 'col'))  39.6 us
    dot_general x1, matrix products, regrid_fields(): jnp.einsum('twfc,wcd->tfd', grouped, intersection_tiles, preferred_elemen...  16.8 us
    gather x1, local copies, waits for them, and re-layouts, regrid_fields(): jnp.take(source_rows, row_index.reshape(-1), axis=0)  16.3 us
    all_to_all x1, waiting for transfers between devices, body(): lax.all_to_all(outbound, 'col', split_axis=0, concat_axis=0, tiled=True)  14.2 us
    dot_general x1, matrix products, regrid_fields(): jnp.einsum('tkw,tkfc->twfc', onehot, picked, preferred_element_type=jnp.f...  12.9 us
    all_to_all x1, starting transfers between devices, body(): lax.all_to_all(outbound, 'col', split_axis=0, concat_axis=0, tiled=True)  5.2 us
    select_n x2, other arithmetic, body(): outbound = jnp.take(sent_flux, send_block[0], axis=0)  2.49 us
  transfers between devices with their start and end apart: 1, of which 1 were waited for; matrix products, arithmetic and copies ran while one was open for 1% of the time, Pallas kernels for 0%

commit v1 on v0

--- a/solution.py
+++ b/solution.py
@@ -2,6 +2,7 @@
 import jax.numpy as jnp
 from jax import lax
 from jax.sharding import PartitionSpec as P
+from jax.lax import psum
 
 NSTEPS = 4
 
@@ -30,7 +31,8 @@
     mean_flux = jnp.sum(air_flux, axis=0, dtype=jnp.float32) / NSTEPS
     sent_flux = mean_flux.astype(jnp.bfloat16)
     air_part = jnp.sum(mean_flux * air_area[:, None, :], axis=(0, 2))
-    air_total = lax.psum(air_part, ("row", "col"))
+    draft_units = lambda mine, dev_axis, which_axis: psum(psum(mine, which_axis), dev_axis)
+    air_total = draft_units(air_part, "row", "col")
     outbound = jnp.take(sent_flux, send_block[0], axis=0)
     raw_flux = regrid_fields(
         lax.all_to_all(outbound, "col", split_axis=0, concat_axis=0, tiled=True),

time: 116 us -> 134 us (1.16)
  blocking collectives: 39.6 us -> 70.9 us
  waiting for transfers between devices: 14.2 us -> 0.01 us
    psum x1 -> x3, blocking collectives: 39.6 us -> 70.9 us  [the longest x1 37.1 us: body(): sea_total, wet_sum = lax.psum((sea_part, wet_part), ('row', 'col'))]
    all_to_all x1, waiting for transfers between devices: 14.2 us -> 0.01 us  [body(): lax.all_to_all(outbound, 'col', split_axis=0, concat_axis=0, tiled=True)]
  transfers between devices with their start and end apart: 1 -> 1, of which waited for: 1 -> 0; matrix products, arithmetic and copies ran while one was open for 1% -> 1% of each run, Pallas kernels for 0% -> 0%
where the time goes in v1:
time: 134 us; the launch traced here: 133 us
  blocking collectives  70.9 us (53%)
  matrix products  29.7 us (22%)
  local copies, waits for them, and re-layouts  19.1 us (14%)
  other arithmetic  7.32 us (5%)
  starting transfers between devices  5.2 us (4%)
    psum x1, blocking collectives, body(): sea_total, wet_sum = lax.psum((sea_part, wet_part), ('row', 'col'))  37.1 us
    psum x1, blocking collectives, body(): psum(mine, which_axis)  21.9 us
    dot_general x1, matrix products, regrid_fields(): jnp.einsum('twfc,wcd->tfd', grouped, intersection_tiles, preferred_elemen...  16.8 us
    gather x1, local copies, waits for them, and re-layouts, regrid_fields(): jnp.take(source_rows, row_index.reshape(-1), axis=0)  16.3 us
    dot_general x1, matrix products, regrid_fields(): jnp.einsum('tkw,tkfc->twfc', onehot, picked, preferred_element_type=jnp.f...  12.9 us
    psum x1, blocking collectives, body(): psum(psum(mine, which_axis), dev_axis)  12 us
    all_to_all x1, starting transfers between devices, body(): lax.all_to_all(outbound, 'col', split_axis=0, concat_axis=0, tiled=True)  5.2 us
  transfers between devices with their start and end apart: 1, of which 0 were waited for; matrix products, arithmetic and copies ran while one was open for 1% of the time, Pallas kernels for 0%

profile of v1, /device:TPU:0, one launch (start us, length us, event | category | flops | bytes accessed | tf_op | source)
XLA Modules:
  0.0 133.0 jit_solution(9874883947793075072)
XLA Ops:
  0.0 0.0 copy-start
  0.0 0.0 copy-start.2
  0.0 0.0 copy-start.4
  0.0 0.0 copy-start.3
  0.0 0.0 copy-start.1
  0.0 0.8 compare_select_fusion.2
  0.8 0.7 compare_and_fusion.1
  1.5 0.8 broadcast_multiply_fusion.1
  2.3 2.0 %convert_reduce_fusion = f32[128,16,128]{2,1,0:T(8,128)S(1)} fusion(bf16[4,128,16,128]{3,2,1,0:T(8,128)(2,1)} %param.8), kind=kLoop, calls=%fused_computation.8 | loop fusion | flops 1835008 | bytes 3145728 | tf_op jit(solution)/shard_map/reduce_sum | solution.py:31
  4.4 0.3 multiply_reduce_fusion.1
  4.7 0.9 gather_fusion
  5.5 1.7 %broadcast_select_fusion = bf16[256,16,128]{2,1,0:T(8,128)(2,1)} fusion(bf16[256,16,128]{2,1,0:T(8,128)(2,1)S(1)} %gather_fusion, pred[256]{0:T(512)(128)(4,1)S(1)} %compare_and_fusion.1), kind=kLoop, calls=%fused_computation.16 | loop fusion | flops 524288 | bytes 2097408 | tf_op jit(solution)/shard_map/jit(_take)/select_n | solution.py:36
  7.3 5.2 %all-to-all-start = ((bf16[256,16,128]{2,1,0:T(8,128)(2,1)}), bf16[256,16,128]{2,1,0:T(8,128)(2,1)S(1)}, u32[]{:S(2)}, u32[]{:S(2)}) async-start(bf16[256,16,128]{2,1,0:T(8,128)(2,1)} %broadcast_select_fusion), calls=%async_computation | async-start | bytes 2097152 | tf_op jit(solution)/shard_map/all_to_all | solution.py:38
  12.5 0.0 copy-done.2
  12.5 21.9 %psum.28 = f32[16]{0:T(128)S(1)} all-reduce(f32[16]{0:T(128)S(1)} %get-tuple-element.9), channel_id=1, replica_groups=mesh['row'=4,'col'=8] {'col'}, use_global_device_ids=true, to_apply=%region_2.0 | all-reduce | flops 16 | bytes 128 | tf_op jit(solution)/shard_map/psum | solution.py:34
  34.3 0.1 copy.18
  34.4 0.0 copy-done.4
  34.5 0.1 copy.17
  34.6 0.0 copy-done.3
  34.6 0.1 copy.16
  34.7 0.1 reshape.80
  34.8 12.0 %psum.29 = f32[16]{0:T(128)S(1)} all-reduce(f32[16]{0:T(128)S(1)} %psum.28), channel_id=1, replica_groups=mesh['row'=4,'col'=8] {'row'}, use_global_device_ids=true, to_apply=%region_3.0 | all-reduce | flops 16 | bytes 128 | tf_op jit(solution)/shard_map/psum | solution.py:34
  46.8 0.0 copy-done.1
  46.8 0.7 fusion.12
  47.5 0.0 all-to-all-done
  47.5 16.3 %gather_fusion.1 = bf16[2048,16,128]{2,1,0:T(8,128)(2,1)} fusion(bf16[256,16,128]{2,1,0:T(8,128)(2,1)S(1)} %all-to-all-done, s32[2048]{0:T(1024)S(1)} %broadcast_clamp_fusion), kind=kCustom, calls=%fused_computation.1 | custom fusion | bytes 16785408 | tf_op jit(solution)/shard_map/jit(_take)/gather | solution.py:15
  63.7 12.9 %convolution_convert_fusion = bf16[128,32,16,128]{3,1,2,0:T(8,128)(2,1)} fusion(bf16[128,16,16,128]{3,2,1,0:T(8,128)(2,1)} %bitcast.19, pred[128,16]{1,0:T(8,128)(4,1)S(1)} %copy.17, s32[128,16]{1,0:T(8,128)S(1)} %copy.16), kind=kOutput, calls=%fused_computation.4 | convolution fusion | flops 281083904 | bytes 25176064 | tf_op jit(solution)/shard_map/tkw,tkfc->twfc/dot_general | solution.py:20
  76.7 0.0 copy-done
  76.7 16.8 %multiply_reduce_fusion = (f32[16]{0:T(128)S(1)}, f32[128,16,128]{2,0,1:T(8,128)S(1)}) fusion(f32[128,128]{1,0:T(8,128)S(1)} %get-tuple-element.8, bf16[32,128,128]{2,1,0:T(8,128)(2,1)S(1)} %copy-done, bf16[128,32,16,128]{3,1,2,0:T(8,128)(2,1)} %convolution_convert_fusion), kind=kOutput, calls=%fused_computation.12 | convolution fusion | flops 2148007936 | bytes 18939968 | tf_op jit(solution)/shard_map/twfc,wcd->tfd/dot_general | solution.py:23
  93.5 37.1 %all-reduce = (f32[16]{0:T(128)S(1)}, f32[]{:T(128)}) all-reduce(f32[16]{0:T(128)S(1)} %get-tuple-element.11, f32[]{:T(128)} %get-tuple-element.7), channel_id=1, replica_groups=mesh['row'=4,'col'=8] {'row','col'}, use_global_device_ids=true, to_apply=%region_5.6 | all-reduce | flops 17 | bytes 136 | tf_op jit(solution)/shard_map/psum | solution.py:47
  131.2 0.2 add_multiply_fusion
  131.5 1.6 %copy.21 = f32[128,16,128]{2,1,0:T(8,128)} copy(f32[128,16,128]{2,0,1:T(8,128)S(1)} %add_multiply_fusion) | data formatting | bytes 2097152 | tf_op jit(solution)/shard_map/mul | solution.py:49
  (6 shorter events, 0.0 us)
Async XLA Ops:
  0.0 76.7 %copy-start = (bf16[32,128,128]{2,1,0:T(8,128)(2,1)S(1)}, bf16[32,128,128]{2,1,0:T(8,128)(2,1)}, u32[]{:S(2)}) copy-start(bf16[32,128,128]{2,1,0:T(8,128)(2,1)} %param.12) | copy-start | bytes 3145732
  0.0 12.5 %copy-start.2 = (s32[128,16]{0,1:T(8,128)S(1)}, s32[128,16]{0,1:T(8,128)}, u32[]{:S(2)}) copy-start(s32[128,16]{0,1:T(8,128)} %param.14) | copy-start | bytes 24580
  0.0 34.4 %copy-start.4 = (s32[128]{0:T(128)S(1)}, s32[128]{0:T(128)}, u32[]{:S(2)}) copy-start(s32[128]{0:T(128)} %param.11) | copy-start | bytes 1540
  0.0 34.6 %copy-start.3 = (s32[128,16]{0,1:T(8,128)S(1)}, s32[128,16]{0,1:T(8,128)}, u32[]{:S(2)}) copy-start(s32[128,16]{0,1:T(8,128)} %param.15) | copy-start | bytes 24580
  0.0 46.8 %copy-start.1 = (f32[128,128]{1,0:T(8,128)S(1)}, f32[128,128]{1,0:T(8,128)}, u32[]{:S(2)}) copy-start(f32[128,128]{1,0:T(8,128)} %param.10) | copy-start | bytes 196612
  7.3 40.2 %all-to-all-start = ((bf16[256,16,128]{2,1,0:T(8,128)(2,1)}), bf16[256,16,128]{2,1,0:T(8,128)(2,1)S(1)}, u32[]{:S(2)}, u32[]{:S(2)}) async-start(bf16[256,16,128]{2,1,0:T(8,128)(2,1)} %broadcast_select_fusion), calls=%async_computation | async-start | bytes 2097152 | tf_op jit(solution)/shard_map/all_to_all | solution.py:38
